TPU v7x, 256 devices: a whole 4x4x8 slice. The times are simulated.
256 devices in a mesh: dp: 4 (over x), expert: 32 (over y, z), tensor: 2 (over core).
Axes of the slice: x: 4, y: 4, z: 8, core: 2. Of those that a mesh axis runs over, the one named last changes fastest.
Arguments:
- tokens: bfloat16 [16384, 2560], P(('dp', 'expert')), may hold values from -6 to 6
- norm_gain: float32 [2560], replicated, may hold values from 0.5 to 1.5
- expert_ids: int32 [16384, 6], P(('dp', 'expert')), may hold values from 0 to 31, all different within a row; in each aligned block of 128 rows (0 to 127, 128 to 255, ...) at most 48 rows name the same one
- route_weights: int32 [16384, 6], P(('dp', 'expert')), may hold values from 1 to 64
- w_gate: bfloat16 [32, 2560, 768], P('expert', None, 'tensor'), may hold values from -0.125 to 0.125
- w_up: bfloat16 [32, 2560, 768], P('expert', None, 'tensor'), may hold values from -0.125 to 0.125
- w_down: bfloat16 [32, 768, 2560], P('expert', 'tensor'), may hold values from -0.21875 to 0.21875
- shared_gate: bfloat16 [2560, 2048], P(None, ('dp', 'tensor')), may hold values from -0.125 to 0.125
- shared_up: bfloat16 [2560, 2048], P(None, ('dp', 'tensor')), may hold values from -0.125 to 0.125
- shared_down: bfloat16 [2048, 2560], P(('dp', 'tensor')), may hold values from -0.125 to 0.125
Outputs:
- mixed: bfloat16 [16384, 2560], P(('dp', 'expert'), 'tensor')
Inputs may be any that keep to these rules, and one draw needn't show every extreme that they name: `expert_ids`: each row names 6 different experts. In each aligned block of 128 rows (the rows of one index of dp+expert) no expert is named by more than 48 rows, a bound that some blocks reach.
All inputs are finite; a program needn't handle non-finite values.
Results may differ from a plain program's by a relative error of at most 0.011.
Values may be sent and summed in bfloat16 or wider, within the bound.
No kernel may reach another device: no remote copies, remote signals or barrier semaphores. Data moves between devices by JAX's collectives and lax.ppermute only.
A program may use at most 128 MiB of HBM per device.

v0:
```python
import jax
import jax.numpy as jnp
from jax import lax
from jax.sharding import PartitionSpec as P

D = 2560
EXPERTS = 32
TOP = 6
CAP = 48
EPSILON = 1e-06


def normalize(tokens, norm_gain):
    values = tokens.astype(jnp.float32)
    inverse = lax.rsqrt(jnp.mean(values * values, axis=1, keepdims=True) + EPSILON)
    return (values * inverse * norm_gain[None, :]).astype(jnp.bfloat16)


def slot_positions(expert_ids):
    flat_ids = expert_ids.reshape(-1)
    onehot = (flat_ids[:, None] == jnp.arange(EXPERTS, dtype=jnp.int32)[None, :]).astype(jnp.int32)
    earlier = jnp.cumsum(onehot, axis=0) - onehot
    return flat_ids * CAP + jnp.sum(earlier * onehot, axis=1)


def on_device(
    tokens,
    norm_gain,
    expert_ids,
    route_weights,
    w_gate,
    w_up,
    w_down,
    shared_gate,
    shared_up,
    shared_down,
):
    normed = normalize(tokens, norm_gain)
    tok_rows = normed.shape[0]
    tensor_count = lax.axis_size("tensor")
    half_width = D // tensor_count
    tensor_rank = lax.axis_index("tensor")
    owners = lax.axis_size("expert")
    exp_local = w_gate.shape[0]
    position = slot_positions(expert_ids)
    pair_count = position.shape[0]
    pair_token = jnp.arange(pair_count, dtype=jnp.int32) // TOP
    filler = jnp.full((EXPERTS * CAP,), -1, jnp.int32).at[position].set(pair_token)
    filled = filler >= 0
    safe_rows = jnp.maximum(filler, 0)
    source_rows = lax.dynamic_slice_in_dim(normed, tensor_rank * half_width, half_width, 1)
    outgoing = jnp.where(filled[:, None], source_rows[safe_rows], jnp.zeros((), jnp.bfloat16))
    outgoing = outgoing.reshape(EXPERTS, CAP, source_rows.shape[1])
    arrived = lax.all_to_all(outgoing, "expert", split_axis=0, concat_axis=0, tiled=True)
    arrived = lax.all_gather(arrived, "tensor", axis=2, tiled=True)
    slot_count = arrived.shape[1]
    grouped = arrived.reshape(owners, exp_local, slot_count, D)
    gate_value = jnp.einsum("jecd,edf->jecf", grouped, w_gate, preferred_element_type=jnp.float32)
    up_value = jnp.einsum("jecd,edf->jecf", grouped, w_up, preferred_element_type=jnp.float32)
    hidden = (jax.nn.silu(gate_value) * up_value).astype(jnp.bfloat16)
    partial_out = jnp.einsum("jecf,efd->jecd", hidden, w_down, preferred_element_type=jnp.float32)
    summed = lax.psum_scatter(
        partial_out.astype(jnp.bfloat16), "tensor", scatter_dimension=3, tiled=True
    )
    summed = summed.reshape(owners * exp_local, slot_count, half_width)
    result_rows = lax.all_to_all(summed, "expert", split_axis=0, concat_axis=0, tiled=True)
    piece_rows = lax.all_gather(normed, "dp", axis=0, tiled=True)
    gate_value = jnp.dot(piece_rows, shared_gate, preferred_element_type=jnp.float32)
    up_value = jnp.dot(piece_rows, shared_up, preferred_element_type=jnp.float32)
    shared_hidden = (jax.nn.silu(gate_value) * up_value).astype(jnp.bfloat16)
    start_row = jnp.int32(0)
    pieces = []
    for offset in range(tok_rows * lax.axis_size(("dp", "tensor")) // tok_rows):
        block_index = start_row // tok_rows + offset
        group_index = block_index // tensor_count
        column_index = block_index % tensor_count
        hidden_block = lax.dynamic_slice_in_dim(shared_hidden, group_index * tok_rows, tok_rows, 0)
        down_block = lax.dynamic_slice_in_dim(shared_down, column_index * half_width, half_width, 1)
        pieces.append(jnp.dot(hidden_block, down_block, preferred_element_type=jnp.float32))
    shared_part = lax.psum_scatter(
        jnp.concatenate(pieces, axis=0).astype(jnp.bfloat16),
        ("dp", "tensor"),
        scatter_dimension=0,
        tiled=True,
    ).astype(jnp.float32)
    table = result_rows.reshape(EXPERTS * CAP, half_width)
    picked = table[position].reshape(tok_rows, TOP, half_width).astype(jnp.float32)
    scales = route_weights.astype(jnp.float32) / 64.0
    routed = jnp.sum(scales[:, :, None] * picked, axis=1)
    return (shared_part + routed).astype(jnp.bfloat16)


def solution(mesh):
    placed = (
        P(("dp", "expert"), None),
        P(),
        P(("dp", "expert"), None),
        P(("dp", "expert"), None),
        P("expert", None, "tensor"),
        P("expert", None, "tensor"),
        P("expert", "tensor", None),
        P(None, ("dp", "tensor")),
        P(None, ("dp", "tensor")),
        P(("dp", "tensor"), None),
    )
    return jax.shard_map(
        on_device,
        mesh=mesh,
        in_specs=placed,
        out_specs=P(("dp", "expert"), "tensor"),
        check_vma=False,
    )
```

profile of v0, /device:TPU:2, one launch (start us, length us, event | category | flops | bytes accessed | tf_op | source)
XLA Modules:
  0.0 321.8 jit_solution(4597402215661047442)
XLA Ops:
  7.4 0.9 copy.14
  8.3 0.1 eq.38
  8.4 0.1 eq.34
  8.6 0.7 broadcast_multiply_fusion
  9.3 1.7 reduce-window.6
  11.0 0.3 slice_reduce_fusion
  11.3 0.1 copy.13
  11.4 0.1 mul.89
  11.6 0.1 fusion.38
  11.7 3.4 %scatter_custom_fusion = s32[1536]{0:T(1024)S(1)} fusion(s32[768]{0:T(1024)S(1)} %fusion.53, s32[768]{0:T(1024)S(1)} %add_select_fusion, s32[]{:T(128)} %constant.415.clone.1), kind=kCustom, calls=%fused_computation.79 | custom fusion | bytes 6148 | tf_op jit(solution)/shard_map/scatter | solution.py:48
  15.2 1.3 fusion.22
  16.5 0.1 broadcast_in_dim.28
  16.6 1.3 fusion.24
  17.9 0.0 copy-start.1
  17.9 6.0 %gather_fusion = bf16[1536,1280]{1,0:T(8,128)(2,1)} fusion(bf16[128,1280]{1,0:T(8,128)(2,1)S(1)} %constant_dynamic-slice_fusion, s32[2048]{0:T(1024)S(1)} %pad_clamp_fusion), kind=kCustom, calls=%fused_computation | custom fusion | bytes 7870464 | tf_op jit(solution)/shard_map/gather | solution.py:52
  24.0 2.4 broadcast_select_fusion
  26.3 101.1 %all_to_all.10 = bf16[32,48,1280]{2,1,0:T(8,128)(2,1)} all-to-all(bf16[32,48,1280]{2,1,0:T(8,128)(2,1)S(1)} %broadcast_select_fusion), channel_id=1, replica_groups=mesh['dp'=4,'expert'=32,'tensor'=2] {'expert'}, dimensions={0} | all-to-all | bytes 7864320 | tf_op jit(solution)/shard_map/all_to_all | solution.py:54
  127.4 0.0 all-gather.5.cloned.1.call-update
  127.5 0.0 reduce-scatter.5.cloned.1.call-start
  127.5 21.8 %all-gather.5.cloned.1.call-done = bf16[32,48,2560]{2,1,0:T(8,128)(2,1)} async-done(((bf16[32,48,1280]{2,1,0:T(8,128)(2,1)}), bf16[32,48,2560]{2,1,0:T(8,128)(2,1)}) %all-gather.5.cloned.1.call-update) | async-done | bytes 7864336 | tf_op jit(solution)/shard_map/all_gather | solution.py:55
  149.3 9.4 %fusion.13 = f32[32,48,384]{2,1,0:T(8,128)} fusion(bf16[32,48,2560]{2,1,0:T(8,128)(2,1)} %all-gather.5.cloned.1.call-done, bf16[1,2560,384]{2,1,0:T(8,128)(2,1)} %param.15), kind=kOutput, calls=%fused_computation.30 | convolution fusion | flops 3019898880 | bytes 12189696 | tf_op jit(solution)/shard_map/jecd,edf->jecf/dot_general | solution.py:59
  158.7 13.5 %convert_bitcast_fusion = bf16[32,1,48,2560]{3,2,0,1:T(8,128)(2,1)} fusion(bf16[1,384,2560]{2,1,0:T(8,128)(2,1)S(1)} %copy-done, f32[32,48,384]{2,1,0:T(8,128)} %fusion.13, bf16[32,48,2560]{2,1,0:T(8,128)(2,1)} %all-gather.5.cloned.1.call-done, bf16[1,2560,384]{2,1,0:T(8,128)(2,1)} %param.14), kind=kOutput, calls=%fused_computation.3 | convolution fusion | flops 6047268864 | bytes 22020096 | tf_op jit(solution)/shard_map/jecf,efd->jecd/dot_general | solution.py:61
  172.3 0.0 reduce-scatter.5.cloned.1.call-update
  172.3 0.0 all-gather.3.cloned.1.call-start
  172.3 0.5 all-gather.3.cloned.1.call-update
  172.9 21.6 %reduce-scatter.5.cloned.1.call-done = bf16[32,1,48,1280]{3,2,0,1:T(8,128)(2,1)} async-done(((bf16[32,1,48,2560]{3,2,0,1:T(8,128)(2,1)}), bf16[32,1,48,1280]{3,2,0,1:T(8,128)(2,1)}) %reduce-scatter.5.cloned.1.call-update) | async-done | bytes 3932176 | tf_op jit(solution)/shard_map/reduce_scatter | solution.py:62
  194.4 10.0 %all-to-all-start.1 = ((bf16[32,48,1280]{2,1,0:T(8,128)(2,1)}), bf16[32,48,1280]{2,1,0:T(8,128)(2,1)}, u32[]{:S(2)}, u32[]{:S(2)}) async-start(bf16[32,48,1280]{2,1,0:T(8,128)(2,1)} %bitcast.91), calls=%async_computation.3 | async-start | bytes 7864320 | tf_op jit(solution)/shard_map/all_to_all | solution.py:66
  204.4 0.2 reduce-scatter.3.cloned.1.call-start
  204.7 7.9 %all-gather.3.cloned.1.call-done = bf16[512,2560]{1,0:T(8,128)(2,1)} async-done(((bf16[128,2560]{1,0:T(8,128)(2,1)}), bf16[512,2560]{1,0:T(8,128)(2,1)}) %all-gather.3.cloned.1.call-update) | async-done | bytes 2621456 | tf_op jit(solution)/shard_map/all_gather | solution.py:67
  212.6 3.1 fusion.55
  215.7 0.0 copy-start.4
  215.7 2.3 fusion.25
  218.0 1.0 fusion.7
  218.9 1.0 fusion.6
  219.9 1.0 fusion.5
  220.9 1.0 fusion.4
  221.9 1.0 fusion.3
  222.9 1.0 fusion.2
  223.9 1.0 fusion.1
  224.9 1.0 fusion
  225.8 0.0 reduce-scatter.3.cloned.1.call-update
  225.9 0.1 copy.12
  226.0 70.2 %all-to-all-done.1 = bf16[32,48,1280]{2,1,0:T(8,128)(2,1)} async-done(((bf16[32,48,1280]{2,1,0:T(8,128)(2,1)}), bf16[32,48,1280]{2,1,0:T(8,128)(2,1)}, u32[]{:S(2)}, u32[]{:S(2)}) %all-to-all-start.1) | async-done | bytes 3932192 | tf_op jit(solution)/shard_map/all_to_all | solution.py:66
  296.2 7.8 %gather_fusion.1 = bf16[768,1280]{1,0:T(8,128)(2,1)} fusion(bf16[1536,1280]{1,0:T(8,128)(2,1)} %bitcast.21, s32[1024]{0:T(1024)S(1)} %pad_clamp_fusion.1), kind=kCustom, calls=%fused_computation.1 | custom fusion | bytes 3935232 | tf_op jit(solution)/shard_map/gather | solution.py:87
  304.0 4.5 %reshape.101 = f32[128,6,1280]{2,1,0:T(8,128)} reshape(bf16[768,1280]{1,0:T(8,128)(2,1)} %gather_fusion.1) | data formatting | bytes 5898240 | tf_op jit(solution)/shard_map/convert_element_type | solution.py:87
  308.5 4.1 %multiply_reduce_fusion = f32[128,1280]{1,0:T(8,128)S(1)} fusion(f32[128,6,1280]{2,1,0:T(8,128)} %reshape.101, f32[128,6]{1,0:T(8,128)S(1)} %copy.12), kind=kLoop, calls=%fused_computation.4 | loop fusion | flops 1802240 | bytes 4590592 | tf_op jit(solution)/shard_map/reduce_sum | solution.py:89
  312.6 0.0 reduce-scatter.3.cloned.1.call-done
  312.7 1.8 add_convert_fusion
  (20 shorter events, 0.1 us)
Async XLA Ops:
  7.4 151.4 %copy-start = (bf16[1,384,2560]{2,1,0:T(8,128)(2,1)S(1)}, bf16[1,384,2560]{2,1,0:T(8,128)(2,1)}, u32[]{:S(2)}) copy-start(bf16[1,384,2560]{2,1,0:T(8,128)(2,1)} %param.16) | copy-start | bytes 5898244
  7.4 141.9 %all-gather.5.cloned.1.call-start = ((), (), s32[]{:S(2)}) async-start(), calls=%async_computation.6 | async-start | bytes 11796480 | tf_op jit(solution)/shard_map/all_gather | solution.py:55
  17.9 6.1 %copy-start.1 = (bf16[128,2560]{1,0:T(8,128)(2,1)}, bf16[128,2560]{1,0:T(8,128)(2,1)S(1)}, u32[]{:S(2)}) copy-start(bf16[128,2560]{1,0:T(8,128)(2,1)S(1)} %fusion.24) | copy-start | bytes 1966084
  127.5 67.0 %reduce-scatter.5.cloned.1.call-start = ((), (), s32[]{:S(2)}) async-start(), calls=%async_computation.7 | async-start | bytes 11796480 | tf_op jit(solution)/shard_map/reduce_scatter | solution.py:62
  172.3 40.3 %all-gather.3.cloned.1.call-start = ((), (), s32[]{:S(2)}) async-start(), calls=%async_computation.4 | async-start | bytes 3276800 | tf_op jit(solution)/shard_map/all_gather | solution.py:67
  194.4 101.8 %all-to-all-start.1 = ((bf16[32,48,1280]{2,1,0:T(8,128)(2,1)}), bf16[32,48,1280]{2,1,0:T(8,128)(2,1)}, u32[]{:S(2)}, u32[]{:S(2)}) async-start(bf16[32,48,1280]{2,1,0:T(8,128)(2,1)} %bitcast.91), calls=%async_computation.3 | async-start | bytes 7864320 | tf_op jit(solution)/shard_map/all_to_all | solution.py:66
  204.4 108.2 %reduce-scatter.3.cloned.1.call-start = ((), (), s32[]{:S(2)}) async-start(), calls=%async_computation.5 | async-start | bytes 2949120 | tf_op jit(solution)/shard_map/reduce_scatter | solution.py:80
  212.6 3.1 copy-start.3
  215.7 2.3 copy-start.4
  223.9 2.0 copy-start.2
Sparse Core Ops, SparseCore 0:
  127.6 21.6 all-gather.4
  172.4 21.9 reduce-scatter.4
Sparse Core Ops, SparseCore 1:
  174.6 37.9 all-gather.2
  225.9 35.7 reduce-scatter.2
where the time goes:
time: 322 us
  waiting for transfers between devices  122 us (38%)
  blocking collectives  101 us (31%)
  matrix products  36.2 us (11%)
  local copies, waits for them, and re-layouts  23.7 us (7%)
  between operations  15.1 us (5%)
  other arithmetic  13.5 us (4%)
  starting transfers between devices  10.3 us (3%)
    all_to_all x1, blocking collectives, on_device(): lax.all_to_all(outgoing, 'expert', split_axis=0, concat_axis=0, tiled=True)  101 us
    all_to_all x1, waiting for transfers between devices, on_device(): lax.all_to_all(summed, 'expert', split_axis=0, concat_axis=0, tiled=True)  70.2 us
    all_gather x1, waiting for transfers between devices, on_device(): arrived = lax.all_gather(arrived, 'tensor', axis=2, tiled=True)  21.8 us
    reduce_scatter x1, waiting for transfers between devices, on_device(): lax.psum_scatter(partial_out.astype(jnp.bfloat16), 'tensor', scatter_dime...  21.6 us
    dot_general x1, matrix products, on_device(): jnp.einsum('jecf,efd->jecd', hidden, w_down, preferred_element_type=jnp.f...  13.5 us
    all_to_all x1, starting transfers between devices, on_device(): lax.all_to_all(summed, 'expert', split_axis=0, concat_axis=0, tiled=True)  9.96 us
    dot_general x1, matrix products, on_device(): jnp.einsum('jecd,edf->jecf', grouped, w_up, preferred_element_type=jnp.fl...  9.41 us
    all_gather x1, waiting for transfers between devices, on_device(): piece_rows = lax.all_gather(normed, 'dp', axis=0, tiled=True)  7.91 us
  transfers between devices with their start and end apart: 5, of which 4 were waited for; matrix products, arithmetic and copies ran while one was open for 9% of the time, Pallas kernels for 0%

commit v1 on v0

--- a/solution.py
+++ b/solution.py
@@ -8,6 +8,14 @@
 TOP = 6
 CAP = 48
 EPSILON = 1e-06
+
+
+def gather_by_exchange(shard, axis, dim):
+    devices = lax.axis_size(axis)
+    repeats = [devices if d == dim else 1 for d in range(shard.ndim)]
+    return lax.all_to_all(
+        jnp.tile(shard, repeats), axis, split_axis=dim, concat_axis=dim, tiled=True
+    )
 
 
 def normalize(tokens, norm_gain):
@@ -52,7 +60,7 @@
     outgoing = jnp.where(filled[:, None], source_rows[safe_rows], jnp.zeros((), jnp.bfloat16))
     outgoing = outgoing.reshape(EXPERTS, CAP, source_rows.shape[1])
     arrived = lax.all_to_all(outgoing, "expert", split_axis=0, concat_axis=0, tiled=True)
-    arrived = lax.all_gather(arrived, "tensor", axis=2, tiled=True)
+    arrived = gather_by_exchange(arrived, "tensor", 2)
     slot_count = arrived.shape[1]
     grouped = arrived.reshape(owners, exp_local, slot_count, D)
     gate_value = jnp.einsum("jecd,edf->jecf", grouped, w_gate, preferred_element_type=jnp.float32)

time: 322 us -> 445 us (1.38); the launches traced: 322 us -> 439 us
  local copies, waits for them, and re-layouts: 23.7 us -> 149 us
  waiting for transfers between devices: 122 us -> 96.4 us
  blocking collectives: 101 us -> 119 us
    unnamed x11 -> x13, local copies, waits for them, and re-layouts: 0.96 us -> 77.1 us
    all_to_all x0 -> x2, local copies, waits for them, and re-layouts: none -> 37.4 us  [the longest x1 22.2 us: gather_by_exchange(): lax.all_to_all(jnp.tile(shard, repeats), axis, split_axis=dim, concat_axi...]
    all_gather x1 -> x0, waiting for transfers between devices: 21.8 us -> none  [on_device(): arrived = lax.all_gather(arrived, 'tensor', axis=2, tiled=True)]
    all_to_all x0 -> x1, blocking collectives: none -> 17.8 us  [gather_by_exchange(): lax.all_to_all(jnp.tile(shard, repeats), axis, split_axis=dim, concat_axi...]
    another operation x0 -> x1, local copies, waits for them, and re-layouts: none -> 11.6 us  [gather_by_exchange(): jnp.tile(shard, repeats)]
  transfers between devices with their start and end apart: 5 -> 4, of which waited for: 4 -> 3; matrix products, arithmetic and copies ran while one was open for 9% -> 7% of each run, Pallas kernels for 0% -> 0%
where the time goes in v1:
time: 445 us; the launch traced here: 439 us
  local copies, waits for them, and re-layouts  149 us (33%)
  blocking collectives  119 us (27%)
  waiting for transfers between devices  96.4 us (22%)
  matrix products  36.2 us (8%)
  between operations  15.3 us (3%)
  other arithmetic  13.5 us (3%)
  starting transfers between devices  10.1 us (2%)
    all_to_all x1, blocking collectives, on_device(): lax.all_to_all(outgoing, 'expert', split_axis=0, concat_axis=0, tiled=True)  101 us
    unnamed x13, local copies, waits for them, and re-layouts  77.1 us
    all_to_all x1, waiting for transfers between devices, on_device(): lax.all_to_all(summed, 'expert', split_axis=0, concat_axis=0, tiled=True)  70.2 us
    all_to_all x1, local copies, waits for them, and re-layouts, gather_by_exchange(): lax.all_to_all(jnp.tile(shard, repeats), axis, split_axis=dim, concat_axi...  22.2 us
    all_to_all x1, blocking collectives, gather_by_exchange(): lax.all_to_all(jnp.tile(shard, repeats), axis, split_axis=dim, concat_axi...  17.8 us
    reduce_scatter x1, waiting for transfers between devices, on_device(): lax.psum_scatter(partial_out.astype(jnp.bfloat16), 'tensor', scatter_dime...  17.6 us
    all_to_all x1, local copies, waits for them, and re-layouts, on_device(): lax.all_to_all(outgoing, 'expert', split_axis=0, concat_axis=0, tiled=True)  15.1 us
    dot_general x1, matrix products, on_device(): jnp.einsum('jecf,efd->jecd', hidden, w_down, preferred_element_type=jnp.f...  13.5 us
  transfers between devices with their start and end apart: 4, of which 3 were waited for; matrix products, arithmetic and copies ran while one was open for 7% of the time, Pallas kernels for 0%

profile of v1, /device:TPU:2, one launch (start us, length us, event | category | flops | bytes accessed | tf_op | source)
XLA Modules:
  0.0 439.5 jit_solution(12934901825076733765)
XLA Ops:
  7.4 0.9 copy.19
  8.3 0.1 eq.38
  8.4 0.1 eq.34
  8.6 0.7 broadcast_multiply_fusion
  9.3 1.7 reduce-window.6
  11.0 0.3 slice_reduce_fusion
  11.3 0.1 copy.18
  11.4 0.1 mul.89
  11.6 0.1 fusion.38
  11.7 3.4 scatter_custom_fusion
  15.2 1.3 fusion.22
  16.5 0.1 broadcast_in_dim.28
  16.6 1.3 fusion.24
  17.9 6.0 %gather_fusion = bf16[1536,1280]{1,0:T(8,128)(2,1)} fusion(bf16[128,1280]{1,0:T(8,128)(2,1)S(1)} %constant_dynamic-slice_fusion, s32[2048]{0:T(1024)S(1)} %pad_clamp_fusion), kind=kCustom, calls=%fused_computation | custom fusion | bytes 7870464 | tf_op jit(solution)/shard_map/gather | solution.py:60
  24.0 2.4 broadcast_select_fusion
  26.3 101.1 %all_to_all.15 = bf16[32,48,1280]{2,1,0:T(8,128)(2,1)} all-to-all(bf16[32,48,1280]{2,1,0:T(8,128)(2,1)S(1)} %broadcast_select_fusion), channel_id=1, replica_groups=mesh['dp'=4,'expert'=32,'tensor'=2] {'expert'}, dimensions={0} | all-to-all | bytes 7864320 | tf_op jit(solution)/shard_map/all_to_all | solution.py:62
  127.4 15.1 %copy.22 = bf16[32,48,1280]{1,0,2:T(8,128)(2,1)} copy(bf16[32,48,1280]{2,1,0:T(8,128)(2,1)} %all_to_all.15) | data formatting | bytes 7864320 | tf_op jit(solution)/shard_map/all_to_all | solution.py:62
  142.6 11.6 %tile.4 = bf16[32,48,2,1280]{1,0,3,2:T(8,128)(2,1)} broadcast(bf16[32,48,1280]{1,0,2:T(8,128)(2,1)} %copy.22), dimensions={0,1,3} | broadcast | bytes 11796480 | tf_op jit(solution)/shard_map/tile | solution.py:17
  154.2 43.9 %reshape.138 = bf16[2,2,983040]{2,1,0:T(2,128)(2,1)} reshape(bf16[2560,32,48]{2,1,0:T(8,128)(2,1)} %bitcast.94) | data formatting | bytes 15728640
  198.0 17.8 %all_to_all.16 = bf16[2,2,983040]{2,1,0:T(2,128)(2,1)} all-to-all(bf16[2,2,983040]{2,1,0:T(2,128)(2,1)} %reshape.138), channel_id=1, replica_groups=mesh['dp'=4,'expert'=32,'tensor'=2] {'tensor'}, dimensions={0} | all-to-all | bytes 15728640 | tf_op jit(solution)/shard_map/all_to_all | solution.py:16
  215.8 32.3 %reshape.139 = bf16[2560,32,48]{2,1,0:T(8,128)(2,1)} reshape(bf16[2,2,983040]{2,1,0:T(2,128)(2,1)} %all_to_all.16) | data formatting | bytes 15728640
  248.1 22.2 %copy.23 = bf16[32,48,2560]{2,1,0:T(8,128)(2,1)} copy(bf16[32,48,2560]{1,0,2:T(8,128)(2,1)} %bitcast.93) | data formatting | bytes 15728640 | tf_op jit(solution)/shard_map/all_to_all | solution.py:16
  270.4 9.5 %fusion.13 = f32[32,48,384]{2,1,0:T(8,128)} fusion(bf16[32,48,2560]{2,1,0:T(8,128)(2,1)} %copy.23, bf16[1,2560,384]{2,1,0:T(8,128)(2,1)} %param.15), kind=kOutput, calls=%fused_computation.30 | convolution fusion | flops 3019898880 | bytes 12189696 | tf_op jit(solution)/shard_map/jecd,edf->jecf/dot_general | solution.py:67
  279.9 13.5 %convert_bitcast_fusion = bf16[32,1,48,2560]{3,2,0,1:T(8,128)(2,1)} fusion(bf16[1,384,2560]{2,1,0:T(8,128)(2,1)S(1)} %copy-done, f32[32,48,384]{2,1,0:T(8,128)} %fusion.13, bf16[32,48,2560]{2,1,0:T(8,128)(2,1)} %copy.23, bf16[1,2560,384]{2,1,0:T(8,128)(2,1)} %param.14), kind=kOutput, calls=%fused_computation.3 | convolution fusion | flops 6047268864 | bytes 22020096 | tf_op jit(solution)/shard_map/jecf,efd->jecd/dot_general | solution.py:69
  293.4 0.0 all-gather.2.cloned.1.call-start
  293.5 0.5 all-gather.2.cloned.1.call-update
  294.0 17.6 %reduce-scatter.5.cloned.1.call-done = bf16[32,1,48,1280]{3,2,0,1:T(8,128)(2,1)} async-done(((bf16[32,1,48,2560]{3,2,0,1:T(8,128)(2,1)}), bf16[32,1,48,1280]{3,2,0,1:T(8,128)(2,1)}) %reduce-scatter.5.cloned.1.call-update) | async-done | bytes 3932176 | tf_op jit(solution)/shard_map/reduce_scatter | solution.py:70
  311.6 10.0 %all-to-all-start.2 = ((bf16[32,48,1280]{2,1,0:T(8,128)(2,1)}), bf16[32,48,1280]{2,1,0:T(8,128)(2,1)}, u32[]{:S(2)}, u32[]{:S(2)}) async-start(bf16[32,48,1280]{2,1,0:T(8,128)(2,1)} %bitcast.96), calls=%async_computation.4 | async-start | bytes 7864320 | tf_op jit(solution)/shard_map/all_to_all | solution.py:74
  321.6 0.0 reduce-scatter.3.cloned.1.call-start
  321.6 8.1 %all-gather.2.cloned.1.call-done = bf16[512,2560]{1,0:T(8,128)(2,1)} async-done(((bf16[128,2560]{1,0:T(8,128)(2,1)}), bf16[512,2560]{1,0:T(8,128)(2,1)}) %all-gather.2.cloned.1.call-update) | async-done | bytes 2621456 | tf_op jit(solution)/shard_map/all_gather | solution.py:75
  329.7 3.1 fusion.55
  332.8 2.3 fusion.25
  335.1 1.0 fusion.7
  336.1 1.0 fusion.6
  337.1 1.0 fusion.5
  338.0 1.0 fusion.4
  339.0 1.0 fusion.3
  340.0 1.0 fusion.2
  341.0 1.0 fusion.1
  342.0 1.0 fusion
  342.9 0.0 reduce-scatter.3.cloned.1.call-update
  343.0 0.1 copy.17
  343.1 70.2 %all-to-all-done.2 = bf16[32,48,1280]{2,1,0:T(8,128)(2,1)} async-done(((bf16[32,48,1280]{2,1,0:T(8,128)(2,1)}), bf16[32,48,1280]{2,1,0:T(8,128)(2,1)}, u32[]{:S(2)}, u32[]{:S(2)}) %all-to-all-start.2) | async-done | bytes 3932192 | tf_op jit(solution)/shard_map/all_to_all | solution.py:74
  413.3 8.1 %gather_fusion.1 = bf16[768,1280]{1,0:T(8,128)(2,1)} fusion(bf16[1536,1280]{1,0:T(8,128)(2,1)} %bitcast.22, s32[1024]{0:T(1024)S(1)} %pad_clamp_fusion.1), kind=kCustom, calls=%fused_computation.1 | custom fusion | bytes 3935232 | tf_op jit(solution)/shard_map/gather | solution.py:95
  421.4 4.5 %reshape.105 = f32[128,6,1280]{2,1,0:T(8,128)} reshape(bf16[768,1280]{1,0:T(8,128)(2,1)} %gather_fusion.1) | data formatting | bytes 5898240 | tf_op jit(solution)/shard_map/convert_element_type | solution.py:95
  425.9 4.1 multiply_reduce_fusion
  430.0 0.0 reduce-scatter.3.cloned.1.call-done
  430.0 1.8 add_convert_fusion
  (23 shorter events, 0.2 us)
Async XLA Ops:
  7.4 272.5 %copy-start = (bf16[1,384,2560]{2,1,0:T(8,128)(2,1)S(1)}, bf16[1,384,2560]{2,1,0:T(8,128)(2,1)}, u32[]{:S(2)}) copy-start(bf16[1,384,2560]{2,1,0:T(8,128)(2,1)} %param.16) | copy-start | bytes 5898244
  7.4 304.2 %reduce-scatter.5.cloned.1.call-start = ((), (), s32[]{:S(2)}) async-start(), calls=%async_computation.7 | async-start | bytes 11796480 | tf_op jit(solution)/shard_map/reduce_scatter | solution.py:70
  17.9 6.1 %copy-start.1 = (bf16[128,2560]{1,0:T(8,128)(2,1)}, bf16[128,2560]{1,0:T(8,128)(2,1)S(1)}, u32[]{:S(2)}) copy-start(bf16[128,2560]{1,0:T(8,128)(2,1)S(1)} %fusion.24) | copy-start | bytes 1966084
  293.4 36.2 %all-gather.2.cloned.1.call-start = ((), (), s32[]{:S(2)}) async-start(), calls=%async_computation.5 | async-start | bytes 3276800 | tf_op jit(solution)/shard_map/all_gather | solution.py:75
  311.6 101.7 %all-to-all-start.2 = ((bf16[32,48,1280]{2,1,0:T(8,128)(2,1)}), bf16[32,48,1280]{2,1,0:T(8,128)(2,1)}, u32[]{:S(2)}, u32[]{:S(2)}) async-start(bf16[32,48,1280]{2,1,0:T(8,128)(2,1)} %bitcast.96), calls=%async_computation.4 | async-start | bytes 7864320 | tf_op jit(solution)/shard_map/all_to_all | solution.py:74
  321.6 108.5 %reduce-scatter.3.cloned.1.call-start = ((), (), s32[]{:S(2)}) async-start(), calls=%async_computation.6 | async-start | bytes 2949120 | tf_op jit(solution)/shard_map/reduce_scatter | solution.py:88
  329.7 3.1 copy-start.3
  332.8 2.3 copy-start.4
  341.0 2.0 copy-start.2
Sparse Core Ops, SparseCore 0:
  293.6 17.9 reduce-scatter.4
Sparse Core Ops, SparseCore 1:
  295.7 33.9 all-gather.1
  343.1 35.7 reduce-scatter.2
